TPU v7x, 8 devices: a whole 2x2x1 slice. The times are simulated.
8 devices in a mesh: rep: 1 (over z), dp: 2 (over y), ad: 4 (over x, core).
Axes of the slice: x: 2, y: 2, z: 1, core: 2. Of those that a mesh axis runs over, the one named last changes fastest.
Arguments:
- x_rows: bfloat16 [16384, 3584], P(('rep', 'dp', 'ad'))
- adapter_id: int32 [16384], P(('rep', 'dp', 'ad'))
- w_gate: bfloat16 [3584, 18944], replicated
- w_up: bfloat16 [3584, 18944], replicated
- w_down: bfloat16 [18944, 3584], replicated
- a_gate: bfloat16 [8, 3584, 64], P('ad')
- b_gate: bfloat16 [8, 64, 18944], P('ad')
- a_up: bfloat16 [8, 3584, 64], P('ad')
- b_up: bfloat16 [8, 64, 18944], P('ad')
- a_down: bfloat16 [8, 18944, 64], P('ad')
- b_down: bfloat16 [8, 64, 3584], P('ad')
Outputs:
- output: bfloat16 [16384, 3584], P(('rep', 'dp', 'ad'))
All inputs are finite; a program needn't handle non-finite values.
Results may differ from a plain program's by a relative error of at most 0.00179.
Values are sent between devices in bfloat16 or wider.
A program may use at most 1.75 GiB of HBM per device.

v0:
```python
import jax
import jax.numpy as jnp
from jax import lax
from jax.sharding import PartitionSpec as P

value_a10 = 32
CAP_MULT = 4


def route_plan(adapter_id, n_rows, group, n_local, capacity):
    owner = adapter_id // n_local
    tok_order = jnp.argsort(owner, stable=True)
    owner_sorted = jnp.take(owner, tok_order)
    counts = jnp.bincount(owner, length=group)
    starts = jnp.cumsum(counts) - counts
    slot_sorted = owner_sorted * capacity + jnp.arange(n_rows) - jnp.take(starts, owner_sorted)
    token_slot = jnp.take(slot_sorted, jnp.argsort(tok_order))
    within = jnp.arange(capacity)
    pick_index = jnp.minimum(starts[:, None] + within[None, :], n_rows - 1).reshape(-1)
    send_rows = jnp.take(tok_order, pick_index)
    filled = (within[None, :] < counts[:, None]).reshape(-1)
    send_local = jnp.where(filled, jnp.take(adapter_id, send_rows) % n_local, 0)
    return token_slot, send_rows, send_local


def solution(mesh):
    group = mesh.shape["ad"]
    tok_axes = ("rep", "dp", "ad")
    row_spec = P(tok_axes, None)
    owned = P("ad", None, None)

    def local_step(x_rows, adapter_id, w_gate, w_up, w_down, a_gate, b_gate, a_up, b_up, a_down, b_down):
        n_rows = x_rows.shape[0]
        n_local, _, rank = a_gate.shape
        d_ff = w_gate.shape[1]
        scale = value_a10 / rank
        capacity = (n_rows // group) * min(CAP_MULT, max(1, group // 2))
        token_slot, send_rows, send_local = route_plan(adapter_id, n_rows, group, n_local, capacity)
        local_recv = lax.all_to_all(send_local, "ad", 0, 0, tiled=True)
        select = (local_recv[:, None] == jnp.arange(n_local)[None, :]).astype(jnp.bfloat16)

        def low_rank(rows_in, a_mat, b_mat):
            low_proj = jnp.einsum("mk,akr->mar", rows_in, a_mat, preferred_element_type=jnp.float32)
            low_proj = low_proj.astype(jnp.bfloat16) * select[:, :, None]
            wide_proj = jnp.einsum("mar,arn->mn", low_proj, b_mat, preferred_element_type=jnp.float32)
            return (scale * wide_proj).astype(jnp.bfloat16)

        x_recv = lax.all_to_all(jnp.take(x_rows, send_rows, axis=0), "ad", 0, 0, tiled=True)
        gu_delta = jnp.concatenate([low_rank(x_recv, a_gate, b_gate), low_rank(x_recv, a_up, b_up)], axis=1)
        gu_token = jnp.take(lax.all_to_all(gu_delta, "ad", 0, 0, tiled=True), token_slot, axis=0)
        gate_pre = jnp.dot(x_rows, w_gate, preferred_element_type=jnp.float32) + gu_token[:, :d_ff].astype(jnp.float32)
        up_proj = jnp.dot(x_rows, w_up, preferred_element_type=jnp.float32) + gu_token[:, d_ff:].astype(jnp.float32)
        hidden = (jax.nn.silu(gate_pre) * up_proj).astype(jnp.bfloat16)
        h_recv = lax.all_to_all(jnp.take(hidden, send_rows, axis=0), "ad", 0, 0, tiled=True)
        down_delta = lax.all_to_all(low_rank(h_recv, a_down, b_down), "ad", 0, 0, tiled=True)
        down_token = jnp.take(down_delta, token_slot, axis=0)
        down_proj = jnp.dot(hidden, w_down, preferred_element_type=jnp.float32) + down_token.astype(jnp.float32)
        return (x_rows.astype(jnp.float32) + down_proj).astype(jnp.bfloat16)

    return jax.shard_map(local_step, mesh=mesh,
                         in_specs=(row_spec, P(tok_axes), P(), P(), P(), owned, owned, owned, owned, owned, owned),
                         out_specs=row_spec, check_vma=False)
```

profile of v0, /device:TPU:0, one launch (start us, length us, event | category | flops | bytes accessed | tf_op | source)
XLA Modules:
  0.0 8088.1 jit_solution(12042021758887211295)
XLA Ops:
  0.8 14.7 scatter_custom_fusion
  16.2 5.0 sort.34
  21.3 23.0 gather_fusion.6
  44.3 19.3 gather_fusion.7
  64.2 4.6 all-to-all-start.1
  68.9 57.8 gather_fusion
  126.7 20.6 broadcast_select_fusion.2
  147.4 9.3 all-to-all-start
  156.7 317.5 %all-to-all-done = bf16[4,1024,3584]{2,1,0:T(8,128)(2,1)} async-done(((bf16[4,1024,3584]{2,1,0:T(8,128)(2,1)}), bf16[4,1024,3584]{2,1,0:T(8,128)(2,1)}, u32[]{:S(2)}, u32[]{:S(2)}) %all-to-all-start) | async-done | bytes 29360160 | tf_op jit(solution)/shard_map/all_to_all | solution.py:48
  474.2 16.2 fusion.29
  490.4 14.8 fusion.28
  505.2 55.8 fusion
  561.0 56.6 fusion.1
  617.6 194.2 %pad_maximum_fusion = bf16[4096,37888]{1,0:T(8,128)(2,1)} fusion(bf16[4096,18944]{1,0:T(8,128)(2,1)} %fusion, bf16[4096,18944]{1,0:T(8,128)(2,1)} %fusion.1), kind=kLoop, calls=%fused_computation.9 | loop fusion | flops 620756992 | bytes 620756992 | tf_op jit(solution)/shard_map/concatenate | solution.py:49
  811.9 53.3 all-to-all-start.2
  865.2 11.8 gather_fusion.4
  877.0 5.0 sort.35
  882.7 2.4 fusion.17
  885.1 11.8 gather_fusion.5
  898.1 301.1 %fusion.27 = f32[2048,18944]{1,0:T(8,128)} fusion(bf16[2048,3584]{1,0:T(8,128)(2,1)} %param.15, bf16[3584,18944]{1,0:T(8,128)(2,1)} %param.17), kind=kOutput, calls=%fused_computation.70 | convolution fusion | flops 278099132416 | bytes 305659904 | tf_op jit(solution)/shard_map/dot_general | solution.py:51
  1199.3 2994.5 %all-to-all-done.2 = bf16[4,1024,37888]{2,1,0:T(8,128)(2,1)} async-done(((bf16[4,1024,37888]{2,1,0:T(8,128)(2,1)}), bf16[4,1024,37888]{2,1,0:T(8,128)(2,1)}, u32[]{:S(2)}, u32[]{:S(2)}) %all-to-all-start.2) | async-done | bytes 310378528 | tf_op jit(solution)/shard_map/all_to_all | solution.py:50
  4193.8 357.2 %gather_fusion.1 = bf16[2048,37888]{1,0:T(8,128)(2,1)} fusion(bf16[4096,37888]{1,0:T(8,128)(2,1)} %bitcast.19, s32[2048]{0:T(1024)S(1)} %copy-done.9), kind=kCustom, calls=%fused_computation.5 | custom fusion | bytes 310386688 | tf_op jit(solution)/shard_map/jit(_take)/gather | solution.py:50
  4551.0 98.8 %broadcast_select_fusion = bf16[2048,37888]{1,0:T(8,128)(2,1)} fusion(bf16[2048,37888]{1,0:T(8,128)(2,1)} %gather_fusion.1, pred[2048]{0:T(1024)(128)(4,1)S(1)} %copy-done.15), kind=kLoop, calls=%fused_computation.15 | loop fusion | flops 77594624 | bytes 310380544 | tf_op jit(solution)/shard_map/jit(_take)/select_n | solution.py:50
  4649.8 339.4 %multiply_convert_fusion = bf16[2048,18944]{1,0:T(8,128)(2,1)} fusion(f32[2048,18944]{1,0:T(8,128)} %fusion.27, bf16[2048,3584]{1,0:T(8,128)(2,1)} %param.15, bf16[3584,18944]{1,0:T(8,128)(2,1)} %param.18, bf16[2048,37888]{1,0:T(8,128)(2,1)} %broadcast_select_fusion), kind=kOutput, calls=%fused_computation.14 | convolution fusion | flops 278487105536 | bytes 538443776 | tf_op jit(solution)/shard_map/dot_general | solution.py:52
  4989.2 509.0 %gather_fusion.2 = bf16[4096,18944]{1,0:T(8,128)(2,1)} fusion(bf16[2048,18944]{1,0:T(8,128)(2,1)} %multiply_convert_fusion, s32[4096]{0:T(1024)S(1)} %copy-done.6), kind=kCustom, calls=%fused_computation.6 | custom fusion | bytes 310394880 | tf_op jit(solution)/shard_map/jit(_take)/gather | solution.py:54
  5498.2 99.0 %broadcast_select_fusion.1 = bf16[4,1024,18944]{2,1,0:T(8,128)(2,1)} fusion(bf16[4,1024,18944]{2,1,0:T(8,128)(2,1)} %bitcast.20, pred[4,1024]{1,0:T(4,128)(4,1)S(1)} %copy-done.12), kind=kLoop, calls=%fused_computation.16 | loop fusion | flops 77594624 | bytes 310382592 | tf_op jit(solution)/shard_map/jit(_take)/select_n | solution.py:54
  5597.3 1735.8 %all_to_all.51 = bf16[4,1024,18944]{2,1,0:T(8,128)(2,1)} all-to-all(bf16[4,1024,18944]{2,1,0:T(8,128)(2,1)} %broadcast_select_fusion.1), channel_id=1, replica_groups=mesh['rep'=1,'dp'=2,'ad'=4] {'ad'}, dimensions={0} | all-to-all | bytes 310378496 | tf_op jit(solution)/shard_map/all_to_all | solution.py:54
  7333.0 58.6 fusion.30
  7391.6 13.6 fusion.2
  7405.2 334.1 %all_to_all.52 = bf16[4,1024,3584]{2,1,0:T(8,128)(2,1)} all-to-all(bf16[4,1024,3584]{2,1,0:T(8,128)(2,1)} %bitcast.77), channel_id=1, replica_groups=mesh['rep'=1,'dp'=2,'ad'=4] {'ad'}, dimensions={0} | all-to-all | bytes 58720256 | tf_op jit(solution)/shard_map/all_to_all | solution.py:55
  7739.3 39.2 gather_fusion.3
  7778.5 309.4 %add_convert_fusion = bf16[2048,3584]{1,0:T(8,128)(2,1)} fusion(bf16[2048,3584]{1,0:T(8,128)(2,1)} %param.15, bf16[2048,18944]{1,0:T(8,128)(2,1)} %multiply_convert_fusion, bf16[18944,3584]{1,0:T(8,128)(2,1)} %param.19, bf16[2048,3584]{1,0:T(8,128)(2,1)} %gather_fusion.3, pred[2048]{0:T(1024)(128)(4,1)S(1)} %copy-done.16), kind=kOutput, calls=%fused_computation.19 | convolution fusion | flops 278143172608 | bytes 257427456 | tf_op jit(solution)/shard_map/dot_general | solution.py:57
  (54 shorter events, 4.1 us)
Async XLA Ops:
  0.0 7391.6 %copy-start = (bf16[2,64,3584]{2,1,0:T(8,128)(2,1)S(1)}, bf16[2,64,3584]{2,1,0:T(8,128)(2,1)}, u32[]{:S(2)}) copy-start(bf16[2,64,3584]{2,1,0:T(8,128)(2,1)} %param.25) | copy-start | bytes 2752516
  0.8 125.9 %copy-start.3 = (s32[2048]{0:T(1024)}, s32[2048]{0:T(1024)S(1)}, u32[]{:S(2)}) copy-start(s32[2048]{0:T(1024)S(1)} %get-tuple-element.14) | copy-start | bytes 24580
  15.7 0.5 copy-start.13
  21.3 105.4 %copy-start.1 = (s32[2048]{0:T(1024)}, s32[2048]{0:T(1024)S(1)}, u32[]{:S(2)}) copy-start(s32[2048]{0:T(1024)S(1)} %get-tuple-element.9) | copy-start | bytes 24580
  44.3 82.4 %copy-start.5 = (s32[4096]{0:T(1024)}, s32[4096]{0:T(1024)S(1)}, u32[]{:S(2)}) copy-start(s32[4096]{0:T(1024)S(1)} %broadcast_clamp_fusion) | copy-start | bytes 49156
  64.2 83.1 %all-to-all-start.1 = ((s32[4,1024,1]{1,2,0:T(1,128)}), s32[4,1024,1]{1,2,0:T(1,128)S(1)}, u32[]{:S(2)}, u32[]{:S(2)}) async-start(s32[4,1024,1]{1,2,0:T(1,128)} %bitcast.11), calls=%async_computation.1 | async-start | bytes 32768 | tf_op jit(solution)/shard_map/all_to_all | solution.py:39
  68.8 57.9 copy-start.11
  126.7 347.5 %copy-start.17 = (bf16[2,3584,64]{1,2,0:T(8,128)(2,1)S(1)}, bf16[2,3584,64]{1,2,0:T(8,128)(2,1)}, u32[]{:S(2)}) copy-start(bf16[2,3584,64]{1,2,0:T(8,128)(2,1)} %param.22) | copy-start | bytes 2752516
  147.4 326.8 %all-to-all-start = ((bf16[4,1024,3584]{2,1,0:T(8,128)(2,1)}), bf16[4,1024,3584]{2,1,0:T(8,128)(2,1)}, u32[]{:S(2)}, u32[]{:S(2)}) async-start(bf16[4,1024,3584]{2,1,0:T(8,128)(2,1)} %broadcast_select_fusion.2), calls=%async_computation | async-start | bytes 58720256 | tf_op jit(solution)/shard_map/all_to_all | solution.py:48
  156.7 404.3 %copy-start.7 = (bf16[4096,2]{0,1:T(2,128)(2,1)}, bf16[4096,2]{0,1:T(2,128)(2,1)S(1)}, u32[]{:S(2)}) copy-start(bf16[4096,2]{0,1:T(2,128)(2,1)S(1)} %compare_convert_fusion) | copy-start | bytes 49156
  811.9 53.3 copy-start.2
  811.9 53.3 copy-start.4
  811.9 70.1 copy-start.14
  811.9 3381.9 %all-to-all-start.2 = ((bf16[4,1024,37888]{2,1,0:T(8,128)(2,1)}), bf16[4,1024,37888]{2,1,0:T(8,128)(2,1)}, u32[]{:S(2)}, u32[]{:S(2)}) async-start(bf16[4,1024,37888]{2,1,0:T(8,128)(2,1)} %bitcast.18), calls=%async_computation.2 | async-start | bytes 620756992 | tf_op jit(solution)/shard_map/all_to_all | solution.py:50
  898.1 3295.7 %copy-start.9 = (s32[2048]{0:T(1024)S(1)}, s32[2048]{0:T(1024)}, u32[]{:S(2)}) copy-start(s32[2048]{0:T(1024)} %broadcast_clamp_fusion.1) | copy-start | bytes 24580
  4193.8 357.2 %copy-start.15 = (pred[2048]{0:T(1024)(128)(4,1)S(1)}, pred[2048]{0:T(1024)(128)(4,1)}, u32[]{:S(2)}) copy-start(pred[2048]{0:T(1024)(128)(4,1)} %compare_and_fusion.1) | copy-start | bytes 6148
  4649.8 339.4 %copy-start.6 = (s32[4096]{0:T(1024)S(1)}, s32[4096]{0:T(1024)}, u32[]{:S(2)}) copy-start(s32[4096]{0:T(1024)} %copy-done.5) | copy-start | bytes 49156
  4989.2 509.0 %copy-start.12 = (pred[4,1024]{1,0:T(4,128)(4,1)S(1)}, pred[4,1024]{1,0:T(4,128)(4,1)}, u32[]{:S(2)}) copy-start(pred[4,1024]{1,0:T(4,128)(4,1)} %copy-done.11) | copy-start | bytes 12292
  7333.0 58.6 copy-start.8
  7391.6 347.7 %copy-start.10 = (s32[2048]{0:T(1024)S(1)}, s32[2048]{0:T(1024)}, u32[]{:S(2)}) copy-start(s32[2048]{0:T(1024)} %broadcast_clamp_fusion.1) | copy-start | bytes 24580
  7739.3 39.2 copy-start.16
where the time goes:
time: 8100 us; the launch traced here: 8090 us
  waiting for transfers between devices  3310 us (41%)
  blocking collectives  2070 us (26%)
  matrix products  1170 us (14%)
  local copies, waits for them, and re-layouts  1030 us (13%)
  other arithmetic  443 us (5%)
    all_to_all x1, waiting for transfers between devices, local_step(): lax.all_to_all(gu_delta, 'ad', 0, 0, tiled=True)  2990 us
    all_to_all x1, blocking collectives, local_step(): lax.all_to_all(jnp.take(hidden, send_rows, axis=0), 'ad', 0, 0, tiled=True)  1740 us
    gather x1, local copies, waits for them, and re-layouts, local_step(): jnp.take(hidden, send_rows, axis=0)  509 us
    gather x1, local copies, waits for them, and re-layouts, local_step(): jnp.take(lax.all_to_all(gu_delta, 'ad', 0, 0, tiled=True), token_slot, ax...  357 us
    dot_general x1, matrix products, local_step(): jnp.dot(x_rows, w_up, preferred_element_type=jnp.float32)  339 us
    all_to_all x1, blocking collectives, local_step(): lax.all_to_all(low_rank(h_recv, a_down, b_down), 'ad', 0, 0, tiled=True)  334 us
    all_to_all x1, waiting for transfers between devices, local_step(): lax.all_to_all(jnp.take(x_rows, send_rows, axis=0), 'ad', 0, 0, tiled=True)  317 us
    dot_general x1, matrix products, local_step(): jnp.dot(hidden, w_down, preferred_element_type=jnp.float32)  309 us
  transfers between devices with their start and end apart: 3, of which 2 were waited for; matrix products, arithmetic and copies ran while one was open for 5% of the time, Pallas kernels for 0%

commit v1 on v0

v1 whole, which is shorter than its diff:
```python
import functools

import jax
import jax.numpy as jnp
from jax import lax
from jax.experimental import pallas as pl
from jax.experimental.pallas import tpu as pltpu
from jax.sharding import PartitionSpec as P

LORA_ALPHA = 32
BLOCK = 512
TILE = 512
HALF = 1024
RAW_BLOCKS = 3
FIRST_BLOCKS = 8
VMEM_BYTES = 66_000_000
F32 = jnp.float32
BF16 = jnp.bfloat16


def dot(a, b):
    return jnp.dot(a, b, preferred_element_type=F32)


def dot_t(a, b):
    return lax.dot_general(a, b, (((1,), (1,)), ((), ())), preferred_element_type=F32)


def rounded(scale, wide):
    return (scale * wide).astype(BF16).astype(F32)


def activation(scale, gate, up, wide_gate, wide_up):
    gate = gate + rounded(scale, wide_gate)
    up = up + rounded(scale, wide_up)
    return (gate * jax.nn.sigmoid(gate) * up).astype(BF16)


def cost(flops, bytes_accessed):
    return pl.CostEstimate(flops=int(flops), bytes_accessed=int(bytes_accessed), transcendentals=0)


def params(semantics):
    return pltpu.CompilerParams(dimension_semantics=semantics, vmem_limit_bytes=VMEM_BYTES)


def base_kernel(x_ref, wg_ref, wu_ref, gate_ref, up_ref):
    def tile(t, _):
        rows = pl.ds(pl.multiple_of(t * TILE, TILE), TILE)
        gate_ref[rows, :] = dot(x_ref[rows, :], wg_ref[...])
        up_ref[rows, :] = dot(x_ref[rows, :], wu_ref[...])
        return 0

    lax.fori_loop(0, x_ref.shape[0] // TILE, tile, 0)


def base_products(x_rows, w_gate, w_up, n_blocks):
    n_rows, d_model = x_rows.shape
    raw = jax.ShapeDtypeStruct((n_rows, n_blocks * BLOCK), F32)
    whole = pl.BlockSpec((n_rows, d_model), lambda j: (0, 0), pipeline_mode=pl.Buffered(1))
    weight = pl.BlockSpec((d_model, BLOCK), lambda j: (0, j))
    block = pl.BlockSpec((n_rows, BLOCK), lambda j: (0, j))
    return pl.pallas_call(
        base_kernel, grid=(n_blocks,), out_shape=(raw, raw), in_specs=[whole, weight, weight],
        out_specs=(block, block), compiler_params=params(("arbitrary",)), name="base_products",
        cost_estimate=cost(4 * n_rows * d_model * n_blocks * BLOCK, 4 * d_model * n_blocks * BLOCK),
    )(x_rows, w_gate, w_up)


def gate_up_kernel(scale, first, aliased, x_ref, wg_ref, wu_ref, lg_ref, lu_ref, bg_ref, bu_ref, *rest):
    if aliased:
        rest = rest[1:]
    h_ref, h_buf, ga, ua, wga, wua, gb, ub, wgb, wub, sems = rest
    j, n_steps = pl.program_id(0), pl.num_programs(0)
    n_tiles = x_ref.shape[0] // TILE
    sets = ((ga, ua, wga, wua), (gb, ub, wgb, wub))

    def copy_out(step):
        cols = pl.ds(pl.multiple_of((first + step) * BLOCK, BLOCK), BLOCK)
        return pltpu.make_async_copy(h_buf.at[step % 2], h_ref.at[:, cols], sems.at[step % 2])

    def products(t, dst):
        rows = pl.ds(pl.multiple_of(t * TILE, TILE), TILE)
        x_t = x_ref[rows, :]
        dst[0][...] = dot(x_t, wg_ref[...])
        dst[1][...] = dot(x_t, wu_ref[...])
        dst[2][...] = dot(lg_ref[rows, :], bg_ref[...])
        dst[3][...] = dot(lu_ref[rows, :], bu_ref[...])

    def finish(src, slot, t):
        chunk = 32
        for r in range(0, TILE, chunk):
            part = pl.ds(r, chunk)
            rows = pl.ds(pl.multiple_of(t * TILE + r, chunk), chunk)
            h_buf[slot, rows, :] = activation(scale, *(s[part, :] for s in src))

    @pl.when(j >= 2)
    def _():
        copy_out(j - 2).wait()

    slot, other = j % 2, (j + 1) % 2
    products(0, sets[0])
    finish(sets[1], other, n_tiles - 1)

    @pl.when(j >= 1)
    def _():
        copy_out(j - 1).start()

    def pair(p, _):
        products(2 * p + 1, sets[1])
        finish(sets[0], slot, 2 * p)
        products(2 * p + 2, sets[0])
        finish(sets[1], slot, 2 * p + 1)
        return 0

    lax.fori_loop(0, n_tiles // 2 - 1, pair, 0)
    products(n_tiles - 1, sets[1])
    finish(sets[0], slot, n_tiles - 2)

    @pl.when(j == n_steps - 1)
    def _():
        finish(sets[1], slot, n_tiles - 1)
        copy_out(j).start()

        @pl.when(j >= 1)
        def _():
            copy_out(j - 1).wait()

        copy_out(j).wait()


def gate_up(scale, x_rows, w_gate, w_up, low, b_mat, first, n_blocks, gate_at, up_at, hidden):
    n_rows, d_model = x_rows.shape
    d_ff, rank = w_gate.shape[1], b_mat.shape[0]
    once = pl.Buffered(1)
    weight = pl.BlockSpec((d_model, BLOCK), lambda j: (0, first + j))
    whole = pl.BlockSpec((n_rows, d_model), lambda j: (0, 0), pipeline_mode=once)
    narrow = pl.BlockSpec((n_rows, rank), lambda j: (0, 0), pipeline_mode=once)
    in_specs = [whole, weight, weight, narrow, narrow,
                pl.BlockSpec((rank, BLOCK), lambda j: (0, gate_at + j)),
                pl.BlockSpec((rank, BLOCK), lambda j: (0, up_at + j))]
    args = [x_rows, w_gate, w_up, low[0], low[1], b_mat, b_mat]
    aliases = {}
    if hidden is not None:
        in_specs.append(pl.BlockSpec(memory_space=pl.ANY))
        aliases = {len(args): 0}
        args.append(hidden)
    width = n_blocks * BLOCK
    return pl.pallas_call(
        functools.partial(gate_up_kernel, scale, first, hidden is not None), grid=(n_blocks,),
        out_shape=jax.ShapeDtypeStruct((n_rows, d_ff), BF16), in_specs=in_specs,
        out_specs=pl.BlockSpec(memory_space=pl.ANY),
        scratch_shapes=[pltpu.VMEM((2, n_rows, BLOCK), BF16)] + [pltpu.VMEM((TILE, BLOCK), F32)] * 8
        + [pltpu.SemaphoreType.DMA((2,))],
        input_output_aliases=aliases, compiler_params=params(("arbitrary",)), name="gate_up",
        cost_estimate=cost(4 * n_rows * (d_model + rank) * width, 4 * d_model * width),
    )(*args)


def finish_kernel(scale, gate_ref, up_ref, lg_ref, lu_ref, bg_ref, bu_ref, hidden_ref, h_ref):
    def tile(t, _):
        rows = pl.ds(pl.multiple_of(t * TILE, TILE), TILE)
        h_ref[rows, :] = activation(scale, gate_ref[rows, :], up_ref[rows, :],
                                    dot(lg_ref[rows, :], bg_ref[...]), dot(lu_ref[rows, :], bu_ref[...]))
        return 0

    lax.fori_loop(0, gate_ref.shape[0] // TILE, tile, 0)


def finish_raw(scale, raw, low, b_mat, gate_at, up_at, hidden):
    n_rows, width = raw[0].shape
    rank = b_mat.shape[0]
    block = pl.BlockSpec((n_rows, BLOCK), lambda j: (0, j))
    narrow = pl.BlockSpec((n_rows, rank), lambda j: (0, 0), pipeline_mode=pl.Buffered(1))
    return pl.pallas_call(
        functools.partial(finish_kernel, scale), grid=(width // BLOCK,),
        out_shape=jax.ShapeDtypeStruct(hidden.shape, BF16),
        in_specs=[block, block, narrow, narrow,
                  pl.BlockSpec((rank, BLOCK), lambda j: (0, gate_at + j)),
                  pl.BlockSpec((rank, BLOCK), lambda j: (0, up_at + j)),
                  pl.BlockSpec(memory_space=pl.ANY)],
        out_specs=block, input_output_aliases={6: 0}, compiler_params=params(("arbitrary",)), name="finish_raw",
        cost_estimate=cost(4 * n_rows * rank * width, 10 * n_rows * width),
    )(raw[0], raw[1], low[0], low[1], b_mat, b_mat, hidden)


def down_kernel(scale, adapter_rank, h_ref, wd_ref, a_ref, b_ref, x_ref, id_ref, out_ref, acc, low_acc):
    k, n_steps = pl.program_id(1), pl.num_programs(1)
    d_model = wd_ref.shape[1]
    tile = 512

    @pl.when(k == 0)
    def _():
        acc[...] = jnp.zeros_like(acc)
        low_acc[...] = jnp.zeros_like(low_acc)

    for m in range(0, HALF, tile):
        rows = pl.ds(m, tile)
        for n in range(0, d_model, tile):
            cols = pl.ds(n, tile)
            acc[rows, cols] += dot(h_ref[rows, :], wd_ref[:, cols])
        low_acc[rows, :] += dot_t(h_ref[rows, :], a_ref[...])

    @pl.when(k == n_steps - 1)
    def _():
        column = lax.broadcasted_iota(jnp.int32, low_acc.shape, 1) // adapter_rank
        low = jnp.where(column == id_ref[...], low_acc[...], 0.0).astype(BF16)
        low_acc[...] = low.astype(F32)

        def part(m, _):
            rows = pl.ds(pl.multiple_of(m * TILE, TILE), TILE)
            low = low_acc[rows, :].astype(BF16)
            for n in range(0, d_model, tile):
                cols = pl.ds(n, tile)
                total = acc[rows, cols] + rounded(scale, dot(low, b_ref[:, cols]))
                out_ref[rows, cols] = (x_ref[rows, cols].astype(F32) + total).astype(BF16)
            return 0

        lax.fori_loop(0, HALF // TILE, part, 0)


def down(scale, adapter_rank, hidden, w_down, adapters, x_rows, slots):
    n_rows, d_model = x_rows.shape
    d_ff, rank = w_down.shape[0], adapters.shape[0]
    once = pl.Buffered(1)
    row_block = pl.BlockSpec((HALF, d_model), lambda i, k: (i, 0), pipeline_mode=once)
    return pl.pallas_call(
        functools.partial(down_kernel, scale, adapter_rank), grid=(n_rows // HALF, d_ff // BLOCK),
        out_shape=jax.ShapeDtypeStruct((n_rows, d_model), BF16),
        in_specs=[pl.BlockSpec((HALF, BLOCK), lambda i, k: (i, k)),
                  pl.BlockSpec((BLOCK, d_model), lambda i, k: (k, 0)),
                  pl.BlockSpec((rank, BLOCK), lambda i, k: (0, d_model // BLOCK + k)),
                  pl.BlockSpec((rank, d_model), lambda i, k: (0, 0), pipeline_mode=once),
                  row_block,
                  pl.BlockSpec((HALF, 1), lambda i, k: (i, 0), pipeline_mode=once)],
        out_specs=pl.BlockSpec((HALF, d_model), lambda i, k: (i, 0)),
        scratch_shapes=[pltpu.VMEM((HALF, d_model), F32), pltpu.VMEM((HALF, rank), F32)],
        compiler_params=params(("arbitrary", "arbitrary")), name="down",
        cost_estimate=cost(2 * n_rows * d_ff * (d_model + rank), 4 * d_ff * d_model),
    )(hidden, w_down, adapters, adapters, x_rows, slots)


def solution(mesh):
    n_dp, n_ad = mesh.shape["dp"], mesh.shape["ad"]
    row_spec = P(("rep", "dp", "ad"), None)
    owned = P("ad", None, None)

    def local_step(x_rows, adapter_id, w_gate, w_up, w_down, a_gate, b_gate, a_up, b_up, a_down, b_down):
        n_local, d_model, rank = a_gate.shape
        d_ff = w_gate.shape[1]
        scale = LORA_ALPHA / rank
        share = n_local // n_dp
        dp = lax.axis_index("dp")

        def mine(mat):
            return lax.dynamic_slice_in_dim(mat, dp * share, share, axis=0)

        def flat(mat):
            return mat.reshape(share * rank, mat.shape[2])

        def gather(parts):
            return lax.all_gather(jnp.concatenate(parts, axis=1), ("dp", "ad"), axis=0, tiled=True)

        owner, local = adapter_id // n_local, adapter_id % n_local
        slots = ((local // share) * n_ad + owner) * share + local % share

        n_all = d_ff // BLOCK
        n_raw, n_first = RAW_BLOCKS, FIRST_BLOCKS
        n_last = n_all - n_raw - n_first
        cut0, cut1 = n_raw * BLOCK, (n_raw + n_first) * BLOCK
        at_gate, at_up, at_down = (flat(jnp.swapaxes(mine(m), 1, 2)) for m in (a_gate, a_up, a_down))
        bt_gate, bt_up, bt_down = (flat(mine(m)) for m in (b_gate, b_up, b_down))

        a_all = gather([at_gate, at_up])
        b_first = gather([bt_gate[:, cut0:cut1], bt_up[:, cut0:cut1]])
        b_last = gather([bt_gate[:, cut1:], bt_gate[:, :cut0], bt_up[:, cut1:], bt_up[:, :cut0]])
        down_all = gather([bt_down, at_down])

        raw = base_products(x_rows, w_gate, w_up, n_raw)
        column = lax.broadcasted_iota(jnp.int32, (x_rows.shape[0], a_all.shape[0]), 1) // rank
        keep = column == slots[:, None]
        low = [jnp.where(keep, dot_t(x_rows, a), 0.0).astype(BF16) for a in (a_all[:, :d_model], a_all[:, d_model:])]
        hidden = gate_up(scale, x_rows, w_gate, w_up, low, b_first, n_raw, n_first, 0, n_first, None)
        hidden = gate_up(scale, x_rows, w_gate, w_up, low, b_last, n_raw + n_first, n_last, 0, n_last + n_raw, hidden)
        hidden = finish_raw(scale, raw, low, b_last, n_last, 2 * n_last + n_raw, hidden)
        return down(scale, rank, hidden, w_down, down_all, x_rows, slots[:, None])

    return jax.shard_map(local_step, mesh=mesh,
                         in_specs=(row_spec, P(("rep", "dp", "ad")), P(), P(), P(), owned, owned, owned, owned, owned, owned),
                         out_specs=row_spec, check_vma=False)
```

time: 8100 us -> 1140 us (0.14)
  waiting for transfers between devices: 3310 us -> 0.09 us
  blocking collectives: 2070 us -> 0 us
  matrix products: 1170 us -> 25.3 us
  Pallas kernels: 0 us -> 1080 us
  local copies, waits for them, and re-layouts: 1030 us -> 11.5 us
  other arithmetic: 443 us -> 5.98 us
    all_to_all x3 -> x0, waiting for transfers between devices: 3310 us -> none  [the longest x1 2990 us: local_step(): lax.all_to_all(gu_delta, 'ad', 0, 0, tiled=True)]
    all_to_all x2 -> x0, blocking collectives: 2070 us -> none  [the longest x1 1740 us: local_step(): lax.all_to_all(jnp.take(hidden, send_rows, axis=0), 'ad', 0, 0, tiled=True)]
    pallas_call x0 -> x5, Pallas kernels: none -> 1080 us  [the longest x2 631 us: gate_up(): pl.pallas_call(functools.partial(gate_up_kernel, scale, first, hidden is...]
    dot_general x6 -> x2, matrix products: 1080 us -> 25.3 us  [dot_t(): lax.dot_general(a, b, (((1,), (1,)), ((), ())), preferred_element_type=F32)]
    gather x9 -> x0, local copies, waits for them, and re-layouts: 1030 us -> none  [the longest x1 509 us: local_step(): jnp.take(hidden, send_rows, axis=0)]
    select_n x4 -> x0, other arithmetic: 219 us -> none  [the longest x1 99 us: local_step(): jnp.take(hidden, send_rows, axis=0)]
    concatenate x1 -> x4, other arithmetic: 194 us -> 5.95 us  [gather(): jnp.concatenate(parts, axis=1)]
    unnamed x3 -> x0, matrix products: 89.6 us -> none
  transfers between devices with their start and end apart: 3 -> 4, of which waited for: 2 -> 0; matrix products, arithmetic and copies ran while one was open for 5% -> 3% of each run, Pallas kernels for 0% -> 62%
where the time goes in v1:
time: 1140 us; the launch traced here: 1130 us
  Pallas kernels  1080 us (95%)
  matrix products  25.3 us (2%)
  between operations  13.7 us (1%)
  local copies, waits for them, and re-layouts  11.5 us (1%)
    pallas_call x2, Pallas kernels, gate_up(): pl.pallas_call(functools.partial(gate_up_kernel, scale, first, hidden is...  631 us
    pallas_call x1, Pallas kernels, down(): pl.pallas_call(functools.partial(down_kernel, scale, adapter_rank), grid=...  369 us
    pallas_call x1, Pallas kernels, base_products(): pl.pallas_call(base_kernel, grid=(n_blocks,), out_shape=(raw, raw), in_sp...  58.3 us
    dot_general x2, matrix products, dot_t(): lax.dot_general(a, b, (((1,), (1,)), ((), ())), preferred_element_type=F32)  25.3 us
  transfers between devices with their start and end apart: 4, of which 0 were waited for; matrix products, arithmetic and copies ran while one was open for 3% of the time, Pallas kernels for 62%

profile of v1, /device:TPU:0, one launch (start us, length us, event | category | flops | bytes accessed | tf_op | source)
XLA Modules:
  0.0 1134.3 jit_solution(3473813480906981437)
XLA Ops:
  6.5 0.0 copy-start
  6.5 1.3 dynamic-slice_bitcast_fusion.4
  7.8 1.1 pad_maximum_fusion.3
  8.9 0.0 all-gather.5.cloned.1.call-update
  8.9 0.0 all-gather.9.cloned.1.call-start
  9.0 2.7 dynamic-slice_bitcast_fusion.1
  11.7 0.0 copy-start.2
  11.7 1.4 copy-done.2
  13.2 1.1 pad_maximum_fusion.2
  14.4 0.0 all-gather.9.cloned.1.call-update
  14.4 0.0 all-gather.7.cloned.1.call-start
  14.4 1.6 slice.34
  16.0 0.1 slice.36
  16.1 0.9 slice.35
  17.1 2.0 pad_maximum_fusion
  19.1 0.0 all-gather.7.cloned.1.call-update
  19.1 0.0 all-gather.11.cloned.1.call-start
  19.2 0.0 copy-done
  19.2 1.8 dynamic-slice_bitcast_fusion
  21.1 0.0 copy-start.3
  21.1 1.7 pad_maximum_fusion.1
  22.8 0.0 all-gather.11.cloned.1.call-update
  22.9 1.4 copy.18.id_ref
  24.3 58.3 %base_products.1 = (f32[2048,1536]{1,0:T(8,128)}, f32[2048,1536]{1,0:T(8,128)}) custom-call(bf16[2048,3584]{1,0:T(8,128)(2,1)} %x_ref.7, bf16[3584,18944]{1,0:T(8,128)(2,1)} %wg_ref.5, bf16[3584,18944]{1,0:T(8,128)(2,1)} %wu_ref.5), custom_call_target="tpu_custom_call" | custom-call | flops 45097156608 | bytes 22020096 | tf_op jit(solution)/shard_map/base_products/pallas_call | solution.py:63
  82.6 13.2 %fusion.lu_ref = bf16[2048,512]{1,0:T(8,128)(2,1)} fusion(bf16[2048,3584]{1,0:T(8,128)(2,1)} %x_ref.7, bf16[512,7168]{1,0:T(8,128)(2,1)} %all-gather.5.cloned.1.call-done, s32[2048]{0:T(1024)S(1)} %fusion.11, s32[512]{0:T(512)S(1)} %get-tuple-element.13, s32[512]{0:T(512)S(1)} %get-tuple-element.14, pred[512]{0:T(512)(128)(4,1)S(1)} %fusion.18), kind=kOutput, calls=%fused_computation.1 | convolution fusion | flops 7520387072 | bytes 20460032 | tf_op jit(solution)/shard_map/dot_general | solution.py:26
  95.8 0.0 copy-done.4
  95.8 12.1 %fusion.1.lg_ref = bf16[2048,512]{1,0:T(8,128)(2,1)} fusion(bf16[2048,3584]{1,0:T(8,128)(2,1)} %x_ref.7, bf16[512,7168]{1,0:T(8,128)(2,1)S(1)} %copy-done.4, s32[2048]{0:T(1024)S(1)} %fusion.11, s32[512]{0:T(512)S(1)} %get-tuple-element.13, s32[512]{0:T(512)S(1)} %get-tuple-element.14, pred[512]{0:T(512)(128)(4,1)S(1)} %fusion.18), kind=kOutput, calls=%fused_computation.3 | convolution fusion | flops 7520387072 | bytes 20460032 | tf_op jit(solution)/shard_map/dot_general | solution.py:26
  107.9 154.9 %gate_up.2.rest_0_ = bf16[2048,18944]{1,0:T(8,128)(2,1)} custom-call(bf16[2048,3584]{1,0:T(8,128)(2,1)} %x_ref.7, bf16[3584,18944]{1,0:T(8,128)(2,1)} %wg_ref.5, bf16[3584,18944]{1,0:T(8,128)(2,1)} %wu_ref.5, bf16[2048,512]{1,0:T(8,128)(2,1)} %fusion.1.lg_ref, bf16[2048,512]{1,0:T(8,128)(2,1)} %fusion.lu_ref, ...), custom_call_target="tpu_custom_call" | custom-call | flops 137438953472 | bytes 58720256 | tf_op jit(solution)/shard_map/gate_up/pallas_call | solution.py:149
  262.8 0.0 all-gather.7.cloned.1.call-done.bg_ref.bu_ref
  262.8 476.3 %gate_up.3.hidden_ref = bf16[2048,18944]{1,0:T(8,128)(2,1)} custom-call(bf16[2048,3584]{1,0:T(8,128)(2,1)} %x_ref.7, bf16[3584,18944]{1,0:T(8,128)(2,1)} %wg_ref.5, bf16[3584,18944]{1,0:T(8,128)(2,1)} %wu_ref.5, bf16[2048,512]{1,0:T(8,128)(2,1)} %fusion.1.lg_ref, bf16[2048,512]{1,0:T(8,128)(2,1)} %fusion.lu_ref, ...), custom_call_target="tpu_custom_call", output_to_operand_aliasing={{}: (7, {})} | custom-call | flops 446676598784 | bytes 190840832 | tf_op jit(solution)/shard_map/gate_up/pallas_call | solution.py:149
  739.2 19.0 %finish_raw.1.h_ref = bf16[2048,18944]{1,0:T(8,128)(2,1)} custom-call(f32[2048,1536]{1,0:T(8,128)} %get-tuple-element.7.gate_ref, f32[2048,1536]{1,0:T(8,128)} %get-tuple-element.8.up_ref, bf16[2048,512]{1,0:T(8,128)(2,1)} %fusion.1.lg_ref, bf16[2048,512]{1,0:T(8,128)(2,1)} %fusion.lu_ref, ...), custom_call_target="tpu_custom_call", output_to_operand_aliasing={{}: (6, {})} | custom-call | flops 6442450944 | bytes 31457280 | tf_op jit(solution)/shard_map/finish_raw/pallas_call | solution.py:175
  758.2 369.1 %down.1 = bf16[2048,3584]{1,0:T(8,128)(2,1)} custom-call(bf16[2048,18944]{1,0:T(8,128)(2,1)} %finish_raw.1.h_ref, bf16[18944,3584]{1,0:T(8,128)(2,1)} %wd_ref.1, bf16[512,22528]{1,0:T(8,128)(2,1)} %all-gather.11.cloned.1.call-done.a_ref.b_ref, bf16[512,22528]{1,0:T(8,128)(2,1)} %all-gather.11.cloned.1.call-done.a_ref.b_ref, bf16[2048,3584]{1,0:T(8,128)(2,1)} %x_ref.7, ...), custom_call_target="tpu_custom_call" | custom-call | flops 317827579904 | bytes 271581184 | tf_op jit(solution)/shard_map/down/pallas_call | solution.py:227
  (15 shorter events, 0.2 us)
Async XLA Ops:
  6.5 12.6 %copy-start = (bf16[2,64,3584]{2,1,0:T(8,128)(2,1)S(1)}, bf16[2,64,3584]{2,1,0:T(8,128)(2,1)}, u32[]{:S(2)}) copy-start(bf16[2,64,3584]{2,1,0:T(8,128)(2,1)} %param.21) | copy-start | bytes 2752516
  6.5 76.0 %all-gather.5.cloned.1.call-start = ((), (), s32[]{:S(2)}) async-start(), calls=%async_computation | async-start | bytes 8257536 | tf_op jit(solution)/shard_map/all_gather | solution.py:262
  8.9 98.9 %all-gather.9.cloned.1.call-start = ((), (), s32[]{:S(2)}) async-start(), calls=%async_computation.2 | async-start | bytes 9437184 | tf_op jit(solution)/shard_map/all_gather | solution.py:262
  11.7 1.4 copy-start.2
  14.4 248.5 %all-gather.7.cloned.1.call-start = ((), (), s32[]{:S(2)}) async-start(), calls=%async_computation.1 | async-start | bytes 34209792 | tf_op jit(solution)/shard_map/all_gather | solution.py:262
  19.1 739.1 %all-gather.11.cloned.1.call-start = ((), (), s32[]{:S(2)}) async-start(), calls=%async_computation.3 | async-start | bytes 25952256 | tf_op jit(solution)/shard_map/all_gather | solution.py:262
  21.1 1.8 copy-start.3
  82.6 13.2 %copy-start.4 = (bf16[512,7168]{1,0:T(8,128)(2,1)S(1)}, bf16[512,7168]{1,0:T(8,128)(2,1)}, u32[]{:S(2)}) copy-start(bf16[512,7168]{1,0:T(8,128)(2,1)} %all-gather.5.cloned.1.call-done) | copy-start | bytes 22020100
  758.2 369.1 %copy-start.1 = (bf16[2,64,3584]{2,1,0:T(8,128)(2,1)S(1)}, bf16[2,64,3584]{2,1,0:T(8,128)(2,1)}, u32[]{:S(2)}) copy-start(bf16[2,64,3584]{2,1,0:T(8,128)(2,1)} %param.21) | copy-start | bytes 2752516
Sparse Core Ops, SparseCore 0:
  9.2 46.7 all-gather.4
  57.8 48.3 all-gather.8
  108.0 141.8 all-gather.6
  251.5 110.7 all-gather.10
